TPU v7x, 32 devices: a whole 2x2x4 slice. The times are simulated.
32 devices in a mesh: grp: 4 (over y, x), brick: 8 (over z, core).
Axes of the slice: x: 2, y: 2, z: 4, core: 2. Of those that a mesh axis runs over, the one named last changes fastest.
Arguments:
- coeffs: bfloat16 [8, 4096, 1024], P(None, 'brick'), may hold values from -6 to 6
- tensor: bfloat16 [32, 1024, 1024], P('grp', 'brick'), may hold values from -0.005859375 to 0.005859375
- pairs: int32 [2, 2], replicated, may hold values from 0 to 7
- lateral: int32 [4096], P('brick'), may hold values from 0 to 511
- thermal: float32 [8], replicated, may hold values from 0.5 to 1
Outputs:
- updated: float32 [32, 8, 4096], P(None, None, 'brick')
Inputs may be any that keep to these rules, and one draw needn't show every extreme that they name: `pairs`: row p names the species that receives the collision term and the species it collides with. A cell's lateral partner, as an index within the same block of 512 cells.
All inputs are finite; a program needn't handle non-finite values.
Results may differ from a plain program's by a relative error of at most 0.0003.
Values may be sent and summed in bfloat16 or wider, within the bound.
A program may use at most 128 MiB of HBM per device.

v0:
```python
import math

import jax
import jax.numpy as jnp
from jax import lax
from jax.experimental import pallas as pl
from jax.experimental.pallas import tpu as pltpu
from jax.sharding import PartitionSpec as P

PLANE = 128

collision_update = 0.5
courant = 0.08
max_speed = 11.0
mixing = 0.2

MESH = pl.DeviceIdType.MESH


def lookup(table, index):
    out = jnp.int32(table[0])
    for i in range(1, len(table)):
        out = jnp.where(index == i, jnp.int32(table[i]), out)
    return out


def fused_kernel(dims, coeffs_ref, tensor_ref, lateral_ref, pairs_ref, thermal_ref, o_ref, *scratch):
    (tbuf, rbuf, lbuf, own_left, win, gathered, hot, part, precv, coll) = scratch[:10]
    views = scratch[10 : 10 + dims["chunks"]]
    (
        chunk_sem,
        t_local,
        t_send,
        t_recv,
        t_side_send,
        t_side_recv,
        r_own_send,
        r_pass_send,
        r_recv,
        r_y_send,
        r_y_recv,
        l_send,
        l_recv,
        l_y_send,
        l_y_recv,
        h_send,
        h_recv,
        p_send,
        p_recv,
        c_send,
        c_recv,
    ) = scratch[10 + dims["chunks"] :]
    line, ways, pieces, subs = dims["line"], dims["ways"], dims["pieces"], dims["subs"]
    chunks, bricks = dims["chunks"], 2 * dims["line"]
    local_modes, depth, width = tensor_ref.shape
    species, cells, _ = coeffs_ref.shape
    modes = local_modes * 2 * ways
    step = local_modes // pieces
    share = cells // ways
    sub = share // subs
    slab = 2 * depth
    layers = cells // PLANE
    per_share = share // PLANE

    g = lax.axis_index("grp")
    b = lax.axis_index("brick")
    x, y = lax.rem(g, 2), lax.div(g, 2)
    z, c = lax.div(b, 2), lax.rem(b, 2)
    other = 1 - c
    nearest = [sorted((q for q in range(line) if q != p), key=lambda q: (abs(q - p), q)) for p in range(line)]
    source = [z] + [lookup([nearest[p][n] for p in range(line)], z) for n in range(line - 1)]
    late = []

    def remote(src, dst, send, recv, tg, tb, when=None):
        copy = pltpu.make_async_remote_copy(
            src_ref=src, dst_ref=dst, send_sem=send, recv_sem=recv, device_id=(tg, tb), device_id_type=MESH
        )
        if when is None:
            copy.start()
        else:
            pl.when(when)(copy.start)
        late.append((copy, when))

    def arrived(dst, recv):
        pltpu.make_async_remote_copy(
            src_ref=dst, dst_ref=dst, send_sem=recv, recv_sem=recv, device_id=(g, b), device_id_type=MESH
        ).wait_recv()

    def share_at(j):
        return lax.rem(y + j, ways)

    for q in range(pieces):
        remote(
            tensor_ref.at[pl.ds(q * step, step)], tbuf.at[x, q, c], t_send.at[q], t_recv.at[q], 2 * y + 1 - x, b
        )
    loads = []
    for j in range(chunks):
        row = pl.multiple_of(share_at(j // per_share) * share + (j % per_share) * PLANE, PLANE)
        copy = pltpu.make_async_copy(coeffs_ref.at[:, pl.ds(row, PLANE)], views[j], chunk_sem.at[j])
        copy.start()
        loads.append(copy)
    own_tensor = []
    for q in range(pieces):
        copy = pltpu.make_async_copy(tensor_ref.at[pl.ds(q * step, step)], tbuf.at[x, q, c], t_local.at[q])
        copy.start()
        own_tensor.append(copy)
        remote(
            tensor_ref.at[pl.ds(q * step, step)],
            tbuf.at[x, q, c],
            t_side_send.at[0, q],
            t_side_recv.at[0, q],
            g,
            2 * z + other,
        )

    receiver, partner = pairs_ref[x, 0], pairs_ref[x, 1]

    for j in range(chunks):
        loads[j].wait()
        if j < per_share:
            part_subs = PLANE // sub
            rbuf[z, y, j * PLANE : (j + 1) * PLANE] = views[j][partner]
            for s in range(j * part_subs, (j + 1) * part_subs):
                rows = pl.ds(s * sub, sub)
                for d, to in enumerate((z - 1, z + 1)):
                    remote(
                        rbuf.at[z, y, rows],
                        rbuf.at[z, y, rows],
                        r_own_send.at[d, s],
                        r_recv.at[z, s],
                        g,
                        2 * to + c,
                        when=(to >= 0) & (to < line),
                    )
        else:
            rbuf[z, share_at(j // per_share), (j % per_share) * PLANE : (j % per_share + 1) * PLANE] = views[j][
                partner
            ]
    for j in range(chunks):
        turned = views[j][receiver].T
        lanes = slice((j % per_share) * PLANE, (j % per_share + 1) * PLANE)
        own_left[:, share_at(j // per_share), :, lanes] = turned.reshape(line, slab, PLANE)
        if j == per_share - 1:
            for n in range(1, line):
                to = source[n]
                remote(own_left.at[to, y], lbuf.at[z, y], l_send.at[n], l_recv.at[z], g, 2 * to + c)
    lbuf[z] = own_left[z]

    wide = -(-modes // PLANE) * PLANE
    for j in range(chunks):
        layer = 1 + share_at(j // per_share) * per_share + j % per_share
        for s in range(species):
            turned = views[j][s, :, :wide].astype(jnp.float32).T
            win[layer, :, s, :] = turned[:modes]
    hot[...] = (lax.broadcasted_iota(jnp.int32, (cells, cells), 0) == lateral_ref[...]).astype(jnp.bfloat16)
    flat = jnp.concatenate(
        [win[1 + i].reshape(modes * species, PLANE).astype(jnp.bfloat16) for i in range(layers)], axis=1
    )
    gathered[...] = jnp.dot(flat, hot[...], preferred_element_type=jnp.float32).reshape(modes, species, cells)
    before, after = lax.rem(b + bricks - 1, bricks), lax.rem(b + 1, bricks)
    remote(win.at[1], win.at[layers + 1], h_send.at[0], h_recv.at[0], g, before)
    remote(win.at[layers], win.at[0], h_send.at[1], h_recv.at[1], g, after)

    def contract(gx, q, zi, yh):
        inner = lax.dot_general(
            tbuf[gx, q].reshape(slab * step, width),
            rbuf[zi, yh],
            (((1,), (1,)), ((), ())),
            preferred_element_type=jnp.float32,
        )
        factor = lbuf[zi, yh].astype(jnp.float32).reshape(2, 1, depth, share)
        terms = inner.reshape(2, step, depth, share) * factor
        sums = jnp.sum(jnp.sum(terms, axis=2), axis=0)
        old = part[zi, gx, yh]
        spots = lax.broadcasted_iota(jnp.int32, old.shape, 0)
        for m in range(step):
            old = jnp.where(spots == q * step + m, sums[m : m + 1], old)
        part[zi, gx, yh] = old

    def block(gx, q_from, q_to, n, j):
        def body(q, carry):
            contract(gx, q, source[n], share_at(j))
            return carry

        lax.fori_loop(q_from, q_to, body, 0)

    ready, pending = [], []

    def run(most):
        for _ in range(min(most, len(pending))):
            pending.pop(0)()

    def rows_ready(n, j):
        pending.append(lambda: block(x, 0, pieces, n, j))
        for q in got:
            pending.append(lambda q=q: block(1 - x, q, q + 1, n, j))
        ready.append((n, j))

    got = []

    def tensor_event(q):
        arrived(tbuf.at[1 - x, q, c], t_recv.at[q])
        remote(
            tbuf.at[1 - x, q, c], tbuf.at[1 - x, q, c], t_side_send.at[1, q], t_side_recv.at[1, q], g, 2 * z + other
        )

    def tensor_ready(q):
        arrived(tbuf.at[1 - x, q, other], t_side_recv.at[1, q])
        for n, j in ready:
            pending.append(lambda n=n, j=j: block(1 - x, q, q + 1, n, j))
        got.append(q)

    def rows_event(n, s):
        src, rows = source[n], pl.ds(s * sub, sub)
        piece = rbuf.at[src, y, rows]
        arrived(piece, r_recv.at[src, s])
        to = jnp.where(src < z, z + 1, z - 1)
        remote(
            piece, piece, r_pass_send.at[n, s], r_recv.at[src, s], g, 2 * to + c, when=(to >= 0) & (to < line)
        )
        for j in range(1, ways):
            remote(piece, piece, r_y_send.at[n, s, j], r_y_recv.at[src, y, s], 2 * share_at(j) + x, b)

    def left_event(n):
        src = source[n]
        arrived(lbuf.at[src, y], l_recv.at[src])
        for j in range(1, ways):
            remote(lbuf.at[src, y], lbuf.at[src, y], l_y_send.at[n, j], l_y_recv.at[src, y], 2 * share_at(j) + x, b)

    def side_event(n, j):
        src, yh = source[n], share_at(j)
        for s in range(subs):
            arrived(rbuf.at[src, yh, pl.ds(s * sub, sub)], r_y_recv.at[src, yh, s])
        arrived(lbuf.at[src, yh], l_y_recv.at[src, yh])

    for copy in own_tensor:
        copy.wait()
    for q in range(pieces):
        arrived(tbuf.at[x, q, other], t_side_recv.at[0, q])
    for j in range(ways):
        rows_ready(0, j)
    run(1)

    events = (line - 1) * subs
    marks = {}
    for q in range(pieces):
        marks.setdefault(min(((q + 1) * events) // pieces, events), []).append(q)
    count = 0
    waiting = []
    for n in range(1, line):
        for s in range(subs):
            rows_event(n, s)
            run(1)
            count += 1
            for q in marks.get(count, []) if count < events else []:
                tensor_event(q)
                run(1)
                tensor_ready(q)
            if s == subs // 2 and waiting:
                for m, j in waiting:
                    side_event(m, j)
                    rows_ready(m, j)
                waiting = []
        left_event(n)
        rows_ready(n, 0)
        waiting = [(n, j) for j in range(1, ways)]
        run(2)
    for q in marks[events]:
        tensor_event(q)
    run(2 * ways)
    for q in marks[events]:
        tensor_ready(q)
    run(len(pending) // 2)
    for m, j in waiting:
        side_event(m, j)
        rows_ready(m, j)
    run(len(pending))

    for n in range(line - 1, 0, -1):
        to = source[n]
        remote(part.at[to], precv.at[z], p_send.at[n], p_recv.at[z], g, 2 * to + c)
    total = part[z]
    for n in range(1, line):
        arrived(precv.at[source[n]], p_recv.at[source[n]])
        total = total + precv[source[n]]
    for gx in range(2):
        for yh in range(ways):
            for i in range(per_share):
                coll[x, y, 1 + yh * per_share + i, gx * local_modes : (gx + 1) * local_modes, :] = total[
                    gx, yh, :, i * PLANE : (i + 1) * PLANE
                ]
    for j in range(2 * ways):
        to = lax.rem(g + j, 2 * ways)
        if j:
            block_ref = coll.at[x, y, pl.ds(1, layers)]
            remote(block_ref, block_ref, c_send.at[0, j], c_recv.at[0, g], to, b)
        remote(coll.at[x, y, 1], coll.at[x, y, layers + 1], c_send.at[1, j], c_recv.at[1, g], to, before)
        remote(coll.at[x, y, layers], coll.at[x, y, 0], c_send.at[2, j], c_recv.at[2, g], to, after)

    arrived(win.at[layers + 1], h_recv.at[0])
    arrived(win.at[0], h_recv.at[1])
    for j in range(2 * ways):
        src = lax.rem(g + j, 2 * ways)
        sx, sy = lax.rem(src, 2), lax.div(src, 2)
        if j:
            arrived(coll.at[sx, sy, pl.ds(1, layers)], c_recv.at[0, src])
        arrived(coll.at[sx, sy, layers + 1], c_recv.at[1, src])
        arrived(coll.at[sx, sy, 0], c_recv.at[2, src])
    for copy, when in late:
        if when is None:
            copy.wait_send()
        else:
            pl.when(when)(copy.wait_send)

    line_of = lax.broadcasted_iota(jnp.int32, (species, PLANE), 0)
    thermo = jnp.zeros((species, PLANE), jnp.float32)
    for s in range(species):
        thermo = jnp.where(line_of == s, thermal_ref[s], thermo)
    chosen = [(line_of == pairs_ref[p, 0]).astype(jnp.float32) for p in range(2)]
    group = 2 * local_modes
    rows = jnp.concatenate(
        [coll[:, :, 1 + i].reshape(2 * ways * group, PLANE) for i in range(layers)], axis=1
    )
    top = rows.astype(jnp.bfloat16)
    rest = rows - top.astype(jnp.float32)
    mid = rest.astype(jnp.bfloat16)
    low = (rest - mid.astype(jnp.float32)).astype(jnp.bfloat16)
    beside = jnp.dot(jnp.concatenate([low, mid, top], axis=0), hot[...], preferred_element_type=jnp.float32)
    count = 2 * ways * group
    beside = beside[:count] + beside[count : 2 * count] + beside[2 * count :]
    zero = jnp.zeros((species, PLANE), jnp.float32)

    def state_of(k):
        if k < 0 or k >= modes:
            return [zero] * (layers + 2)
        out = []
        for i in range(layers + 2):
            add = zero
            for p in range(2):
                add = add + chosen[p] * coll[p, k // group, i, k % group : k % group + 1, :]
            out.append(win[i, k] + collision_update * add)
        return out

    below, middle = state_of(-1), state_of(0)
    for k in range(modes):
        above = state_of(k + 1)
        speed = [
            thermo * (math.sqrt(k) * below[i] + math.sqrt(k + 1.0) * above[i]) for i in range(layers + 2)
        ]
        face = [
            0.5 * (speed[i] + speed[i + 1]) - 0.5 * max_speed * thermo * (middle[i + 1] - middle[i])
            for i in range(layers + 1)
        ]
        for i in range(layers):
            lanes = slice(i * PLANE, (i + 1) * PLANE)
            add = zero
            for p in range(2):
                row = p * ways * group + k
                add = add + chosen[p] * beside[row : row + 1, lanes]
            partner_state = gathered[k, :, lanes] + collision_update * add
            center = middle[i + 1]
            o_ref[k, :, lanes] = (
                center - courant * (face[i + 1] - face[i]) + mixing * (partner_state - center)
            )
        below, middle = middle, above


def local(coeffs, tensor, pairs, lateral, thermal):
    species, cells, width = coeffs.shape
    local_modes, depth, _ = tensor.shape
    bricks, groups = lax.axis_size("brick"), lax.axis_size("grp")
    assert pairs.shape[0] == 2 and bricks % 2 == 0 and groups % 2 == 0
    line, ways = bricks // 2, groups // 2
    modes = local_modes * groups
    share = cells // ways
    assert share % PLANE == 0 and width == bricks * depth
    step = 2 if local_modes % 2 == 0 else 1
    pieces = local_modes // step
    subs = share // 64
    chunks = cells // PLANE
    layers = cells // PLANE
    slab = 2 * depth
    dims = dict(line=line, ways=ways, pieces=pieces, subs=subs, chunks=chunks)
    bf16, f32 = jnp.bfloat16, jnp.float32
    sem = pltpu.SemaphoreType.DMA
    scratch = [
        pltpu.VMEM((2, pieces, 2, step, depth, width), bf16),
        pltpu.VMEM((line, ways, share, width), bf16),
        pltpu.VMEM((line, ways, slab, share), bf16),
        pltpu.VMEM((line, ways, slab, share), bf16),
        pltpu.VMEM((layers + 2, modes, species, PLANE), f32),
        pltpu.VMEM((modes, species, cells), f32),
        pltpu.VMEM((cells, cells), bf16),
        pltpu.VMEM((line, 2, ways, local_modes, share), f32),
        pltpu.VMEM((line, 2, ways, local_modes, share), f32),
        pltpu.VMEM((2, ways, layers + 2, 2 * local_modes, PLANE), f32),
    ]
    scratch += [pltpu.VMEM((species, PLANE, width), bf16)] * chunks
    scratch += [
        sem((chunks,)),
        sem((pieces,)),
        sem((pieces,)),
        sem((pieces,)),
        sem((2, pieces)),
        sem((2, pieces)),
        sem((2, subs)),
        sem((line, subs)),
        sem((line, subs)),
        sem((line, subs, ways)),
        sem((line, ways, subs)),
        sem((line,)),
        sem((line,)),
        sem((line, ways)),
        sem((line, ways)),
        sem((2,)),
        sem((2,)),
        sem((line,)),
        sem((line,)),
        sem((3, groups)),
        sem((3, groups)),
    ]
    return pl.pallas_call(
        lambda *refs: fused_kernel(dims, *refs),
        out_shape=jax.ShapeDtypeStruct((modes, species, cells), f32),
        in_specs=[
            pl.BlockSpec(memory_space=pl.ANY),
            pl.BlockSpec(memory_space=pl.ANY),
            pl.BlockSpec(memory_space=pltpu.VMEM),
            pl.BlockSpec(memory_space=pltpu.SMEM),
            pl.BlockSpec(memory_space=pltpu.SMEM),
        ],
        out_specs=pl.BlockSpec(memory_space=pltpu.VMEM),
        scratch_shapes=scratch,
        compiler_params=pltpu.CompilerParams(has_side_effects=True, vmem_limit_bytes=60 * 2**20),
        name="fused",
    )(coeffs, tensor, lateral.reshape(1, cells), pairs, thermal)


def solution(mesh):
    in_specs = (P(None, "brick", None), P("grp", "brick", None), P(), P("brick"), P())
    out_specs = P(None, None, "brick")
    return jax.shard_map(local, mesh=mesh, in_specs=in_specs, out_specs=out_specs, check_vma=False)
```

profile of v0, /device:TPU:0, one launch (start us, length us, event | category | flops | bytes accessed | tf_op | source)
XLA Modules:
  0.0 87.2 jit_solution(4477232889462728937)
XLA Ops:
  0.0 85.3 %fused.1 = f32[32,8,512]{2,1,0:T(8,128)} custom-call(bf16[8,512,1024]{2,1,0:T(8,128)(2,1)} %refs_0_.1, bf16[8,128,1024]{2,1,0:T(8,128)(2,1)} %refs_1_.1, s32[1,512]{1,0:T(1,128)} %bitcast.1, s32[2,2]{1,0:T(2,128)} %refs_3_.1, f32[8]{0:T(128)} %refs_4_.1), custom_call_target="tpu_custom_call" | custom-call | tf_op jit(solution)/shard_map/fused/pallas_call | solution.py:422
  85.3 1.9 %copy.7 = f32[32,8,512]{2,1,0:T(8,128)} copy(f32[32,8,512]{2,1,0:T(8,128)} %fused.1) | data formatting | bytes 1048576
where the time goes:
time: 87.6 us; the launch traced here: 87.2 us
  Pallas kernels  85.3 us (97%)
  local copies, waits for them, and re-layouts  1.87 us (2%)
    pallas_call x1, Pallas kernels, local(): pl.pallas_call(lambda *refs: fused_kernel(dims, *refs), out_shape=jax.Sha...  85.3 us
    unnamed x1, local copies, waits for them, and re-layouts  1.87 us

commit v1 on v0

--- a/solution.py
+++ b/solution.py
@@ -57,7 +57,7 @@
     modes = local_modes * 2 * ways
     step = local_modes // pieces
     share = cells // ways
-    sub = share // subs
+    sub = width // subs
     slab = 2 * depth
     layers = cells // PLANE
     per_share = share // PLANE
@@ -69,6 +69,8 @@
     other = 1 - c
     nearest = [sorted((q for q in range(line) if q != p), key=lambda q: (abs(q - p), q)) for p in range(line)]
     source = [z] + [lookup([nearest[p][n] for p in range(line)], z) for n in range(line - 1)]
+    away = [jnp.abs(source[n] - z) for n in range(line)]
+    gaps = [sorted({abs(nearest[p][n - 1] - p) for p in range(line)}) if n else [0] for n in range(line)]
     late = []
 
     def remote(src, dst, send, recv, tg, tb, when=None):
@@ -89,21 +91,30 @@
     def share_at(j):
         return lax.rem(y + j, ways)
 
+    before, after = lax.rem(b + bricks - 1, bricks), lax.rem(b + 1, bricks)
+    loads = []
+    for j in range(chunks):
+        row = pl.multiple_of(share_at(j // per_share) * share + (j % per_share) * PLANE, PLANE)
+        loads.append(pltpu.make_async_copy(coeffs_ref.at[:, pl.ds(row, PLANE)], views[j], chunk_sem.at[j]))
+    for j in range(per_share):
+        loads[j].start()
+    barrier = pltpu.get_barrier_semaphore()
+    peers = [(lax.rem(g + j, 2 * ways), b) for j in range(1, 2 * ways)]
+    peers += [(lax.rem(g + j, 2 * ways), to) for j in range(2 * ways) for to in (before, after)]
+    peers += [(g, 2 * source[n] + c) for n in range(1, line)]
+    for peer in peers:
+        pl.semaphore_signal(barrier, inc=1, device_id=peer, device_id_type=MESH)
+    pl.semaphore_wait(barrier, len(peers))
+
     for q in range(pieces):
         remote(
             tensor_ref.at[pl.ds(q * step, step)], tbuf.at[x, q, c], t_send.at[q], t_recv.at[q], 2 * y + 1 - x, b
         )
-    loads = []
-    for j in range(chunks):
-        row = pl.multiple_of(share_at(j // per_share) * share + (j % per_share) * PLANE, PLANE)
-        copy = pltpu.make_async_copy(coeffs_ref.at[:, pl.ds(row, PLANE)], views[j], chunk_sem.at[j])
-        copy.start()
-        loads.append(copy)
     own_tensor = []
     for q in range(pieces):
-        copy = pltpu.make_async_copy(tensor_ref.at[pl.ds(q * step, step)], tbuf.at[x, q, c], t_local.at[q])
-        copy.start()
-        own_tensor.append(copy)
+        own_tensor.append(
+            pltpu.make_async_copy(tensor_ref.at[pl.ds(q * step, step)], tbuf.at[x, q, c], t_local.at[q])
+        )
         remote(
             tensor_ref.at[pl.ds(q * step, step)],
             tbuf.at[x, q, c],
@@ -115,88 +126,139 @@
 
     receiver, partner = pairs_ref[x, 0], pairs_ref[x, 1]
 
-    for j in range(chunks):
+    def lanes_of(j):
+        return slice((j % per_share) * PLANE, (j % per_share + 1) * PLANE)
+
+    def turn_rows(j, s):
+        span = slice(s * sub, (s + 1) * sub)
+        rbuf[z, share_at(j // per_share), span, lanes_of(j)] = views[j][partner, :, span].T
+
+    def turn_left(j):
+        own_left[:, share_at(j // per_share), :, lanes_of(j)] = views[j][receiver].T.reshape(line, slab, PLANE)
+
+    for j in range(per_share):
         loads[j].wait()
-        if j < per_share:
-            part_subs = PLANE // sub
-            rbuf[z, y, j * PLANE : (j + 1) * PLANE] = views[j][partner]
-            for s in range(j * part_subs, (j + 1) * part_subs):
-                rows = pl.ds(s * sub, sub)
-                for d, to in enumerate((z - 1, z + 1)):
-                    remote(
-                        rbuf.at[z, y, rows],
-                        rbuf.at[z, y, rows],
-                        r_own_send.at[d, s],
-                        r_recv.at[z, s],
-                        g,
-                        2 * to + c,
-                        when=(to >= 0) & (to < line),
-                    )
-        else:
-            rbuf[z, share_at(j // per_share), (j % per_share) * PLANE : (j % per_share + 1) * PLANE] = views[j][
-                partner
-            ]
-    for j in range(chunks):
-        turned = views[j][receiver].T
-        lanes = slice((j % per_share) * PLANE, (j % per_share + 1) * PLANE)
-        own_left[:, share_at(j // per_share), :, lanes] = turned.reshape(line, slab, PLANE)
-        if j == per_share - 1:
-            for n in range(1, line):
-                to = source[n]
-                remote(own_left.at[to, y], lbuf.at[z, y], l_send.at[n], l_recv.at[z], g, 2 * to + c)
-    lbuf[z] = own_left[z]
+    for copy in loads[per_share:] + own_tensor:
+        copy.start()
+    lead = subs // 2
+    slots = [lead + (n - 1) * (subs - lead) // (line - 1) for n in range(1, line)]
+    for s in range(subs):
+        for j in range(per_share):
+            turn_rows(j, s)
+        if s == lead:
+            for j in range(per_share):
+                turn_left(j)
+        for n in range(1, line):
+            if slots[n - 1] == s:
+                to = 2 * source[n] + c
+                remote(own_left.at[source[n], y], lbuf.at[z, y], l_send.at[n], l_recv.at[z], g, to)
+        piece = rbuf.at[z, y, pl.ds(s * sub, sub)]
+        for d, to in enumerate((z - 1, z + 1)):
+            remote(
+                piece, piece, r_own_send.at[d, s], r_recv.at[z, s], g, 2 * to + c, when=(to >= 0) & (to < line)
+            )
+
+    def other_shares():
+        for j in range(per_share, chunks):
+            loads[j].wait()
+            for s in range(subs):
+                turn_rows(j, s)
+            turn_left(j)
+        lbuf[z] = own_left[z]
 
     wide = -(-modes // PLANE) * PLANE
-    for j in range(chunks):
+
+    def window_task(j):
         layer = 1 + share_at(j // per_share) * per_share + j % per_share
         for s in range(species):
             turned = views[j][s, :, :wide].astype(jnp.float32).T
             win[layer, :, s, :] = turned[:modes]
-    hot[...] = (lax.broadcasted_iota(jnp.int32, (cells, cells), 0) == lateral_ref[...]).astype(jnp.bfloat16)
-    flat = jnp.concatenate(
-        [win[1 + i].reshape(modes * species, PLANE).astype(jnp.bfloat16) for i in range(layers)], axis=1
-    )
-    gathered[...] = jnp.dot(flat, hot[...], preferred_element_type=jnp.float32).reshape(modes, species, cells)
-    before, after = lax.rem(b + bricks - 1, bricks), lax.rem(b + 1, bricks)
-    remote(win.at[1], win.at[layers + 1], h_send.at[0], h_recv.at[0], g, before)
-    remote(win.at[layers], win.at[0], h_send.at[1], h_recv.at[1], g, after)
-
-    def contract(gx, q, zi, yh):
-        inner = lax.dot_general(
-            tbuf[gx, q].reshape(slab * step, width),
-            rbuf[zi, yh],
-            (((1,), (1,)), ((), ())),
-            preferred_element_type=jnp.float32,
-        )
-        factor = lbuf[zi, yh].astype(jnp.float32).reshape(2, 1, depth, share)
-        terms = inner.reshape(2, step, depth, share) * factor
-        sums = jnp.sum(jnp.sum(terms, axis=2), axis=0)
-        old = part[zi, gx, yh]
-        spots = lax.broadcasted_iota(jnp.int32, old.shape, 0)
-        for m in range(step):
-            old = jnp.where(spots == q * step + m, sums[m : m + 1], old)
-        part[zi, gx, yh] = old
-
-    def block(gx, q_from, q_to, n, j):
-        def body(q, carry):
-            contract(gx, q, source[n], share_at(j))
-            return carry
-
-        lax.fori_loop(q_from, q_to, body, 0)
-
-    ready, pending = [], []
-
-    def run(most):
-        for _ in range(min(most, len(pending))):
-            pending.pop(0)()
+
+    def lateral_task():
+        hot[...] = (lax.broadcasted_iota(jnp.int32, (cells, cells), 0) == lateral_ref[...]).astype(jnp.bfloat16)
+        flat = jnp.concatenate(
+            [win[1 + i].reshape(modes * species, PLANE).astype(jnp.bfloat16) for i in range(layers)], axis=1
+        )
+        gathered[...] = jnp.dot(flat, hot[...], preferred_element_type=jnp.float32).reshape(modes, species, cells)
+
+    def halo_task():
+        remote(win.at[1], win.at[layers + 1], h_send.at[0], h_recv.at[0], g, before)
+        remote(win.at[layers], win.at[0], h_send.at[1], h_recv.at[1], g, after)
+
+    def contract(gx, q, count, zi, yh):
+        halves = []
+        for half in range(2):
+            inner = jnp.dot(
+                tbuf[gx, pl.ds(q, count), half].reshape(count * step * depth, width),
+                rbuf[zi, yh],
+                preferred_element_type=jnp.float32,
+            )
+            factor = lbuf[zi, yh, half * depth : (half + 1) * depth].astype(jnp.float32)
+            terms = inner.reshape(count * step, depth, share) * factor[None]
+            halves.append(jnp.sum(terms, axis=1))
+        return halves[0] + halves[1]
+
+    def block(gx, q, count, n, j):
+        zi, yh = source[n], share_at(j)
+        part[zi, gx, yh, q * step : (q + count) * step, :] = contract(gx, q, count, zi, yh)
+
+    done = {}
+
+    def finished(kind, n, j, count):
+        done[kind, n, j] = done.get((kind, n, j), 0) + count
+        if n and done[kind, n, j] == pieces:
+            gx, yh, to = (x, 1 - x)[kind], share_at(j), source[n]
+            remote(part.at[to, gx, yh], precv.at[z, gx, yh], p_send.at[n, kind, j], p_recv.at[z, gx, yh], g, 2 * to + c)
+
+    def work(kind, q, count, n, j):
+        def go():
+            block((x, 1 - x)[kind], q, count, n, j)
+            finished(kind, n, j, count)
+
+        return (count * 0.09 + 0.06, go)
+
+    wire = 92e3
+    piece_us = 2 * share * width * 2 / wire
+    left_us = 2 * slab * share * 2 / wire
+    tensor_us = 2 * step * depth * width * 2 / wire
+    begin, hop, side_hop = 0.7, 2.6, 3.4
+    sub_us = piece_us / subs
+    agenda = []
+    for n in range(1, line):
+        left_at = begin + slots[n - 1] * sub_us + 2 * n * left_us
+        agenda.append((left_at, "left", n, 0, 0))
+        last = 0.0
+        for gap in gaps[n]:
+            for s in range(subs):
+                at = begin + (gap - 1) * piece_us + (s + 1) * sub_us
+                if gap == 1:
+                    at += left_us * sum(s >= slot for slot in slots[:2])
+                elif gap == 2:
+                    at += left_us * (2 + (line - 3) * (s + 1) / subs)
+                else:
+                    at += left_us * (line - 1)
+                agenda.append((at, "rows", n, s, gap))
+            last = at
+        agenda.append((max(last, left_at) + 0.01, "own", n, 0, 0))
+        for j in range(1, ways):
+            agenda.append((max(last, left_at) + sub_us + hop + 2.0, "side", n, j, 0))
+    for q in range(pieces):
+        agenda.append((hop + (q + 1) * tensor_us, "tensor", q, 0, 0))
+        agenda.append((hop + (q + 1) * tensor_us + side_hop, "tensor_side", q, 0, 0))
+    agenda.sort(key=lambda item: item[0])
+
+    pending, got, ready = [], [], []
+    half = max(1, pieces // 2)
 
     def rows_ready(n, j):
-        pending.append(lambda: block(x, 0, pieces, n, j))
-        for q in got:
-            pending.append(lambda q=q: block(1 - x, q, q + 1, n, j))
+        for q in range(0, pieces, half):
+            pending.append(work(0, q, half, n, j))
+        run_from = 0
+        while run_from < len(got):
+            count = min(half, len(got) - run_from)
+            pending.append(work(1, run_from, count, n, j))
+            run_from += count
         ready.append((n, j))
-
-    got = []
 
     def tensor_event(q):
         arrived(tbuf.at[1 - x, q, c], t_recv.at[q])
@@ -207,19 +269,28 @@
     def tensor_ready(q):
         arrived(tbuf.at[1 - x, q, other], t_side_recv.at[1, q])
         for n, j in ready:
-            pending.append(lambda n=n, j=j: block(1 - x, q, q + 1, n, j))
+            pending.append(work(1, q, 1, n, j))
         got.append(q)
 
-    def rows_event(n, s):
-        src, rows = source[n], pl.ds(s * sub, sub)
-        piece = rbuf.at[src, y, rows]
-        arrived(piece, r_recv.at[src, s])
+    def rows_event(n, s, gap):
+        src = source[n]
+        piece = rbuf.at[src, y, pl.ds(s * sub, sub)]
+        near = away[n] == gap
+        pl.when(near)(lambda: arrived(piece, r_recv.at[src, s]))
         to = jnp.where(src < z, z + 1, z - 1)
         remote(
-            piece, piece, r_pass_send.at[n, s], r_recv.at[src, s], g, 2 * to + c, when=(to >= 0) & (to < line)
+            piece,
+            piece,
+            r_pass_send.at[n, s],
+            r_recv.at[src, s],
+            g,
+            2 * to + c,
+            when=near & (to >= 0) & (to < line),
         )
         for j in range(1, ways):
-            remote(piece, piece, r_y_send.at[n, s, j], r_y_recv.at[src, y, s], 2 * share_at(j) + x, b)
+            remote(
+                piece, piece, r_y_send.at[n, s, j], r_y_recv.at[src, y, s], 2 * share_at(j) + x, b, when=near
+            )
 
     def left_event(n):
         src = source[n]
@@ -233,55 +304,52 @@
             arrived(rbuf.at[src, yh, pl.ds(s * sub, sub)], r_y_recv.at[src, yh, s])
         arrived(lbuf.at[src, yh], l_y_recv.at[src, yh])
 
-    for copy in own_tensor:
-        copy.wait()
-    for q in range(pieces):
-        arrived(tbuf.at[x, q, other], t_side_recv.at[0, q])
-    for j in range(ways):
-        rows_ready(0, j)
-    run(1)
-
-    events = (line - 1) * subs
-    marks = {}
-    for q in range(pieces):
-        marks.setdefault(min(((q + 1) * events) // pieces, events), []).append(q)
-    count = 0
-    waiting = []
-    for n in range(1, line):
-        for s in range(subs):
-            rows_event(n, s)
-            run(1)
-            count += 1
-            for q in marks.get(count, []) if count < events else []:
-                tensor_event(q)
-                run(1)
-                tensor_ready(q)
-            if s == subs // 2 and waiting:
-                for m, j in waiting:
-                    side_event(m, j)
-                    rows_ready(m, j)
-                waiting = []
-        left_event(n)
-        rows_ready(n, 0)
-        waiting = [(n, j) for j in range(1, ways)]
-        run(2)
-    for q in marks[events]:
-        tensor_event(q)
-    run(2 * ways)
-    for q in marks[events]:
-        tensor_ready(q)
-    run(len(pending) // 2)
-    for m, j in waiting:
-        side_event(m, j)
-        rows_ready(m, j)
-    run(len(pending))
-
-    for n in range(line - 1, 0, -1):
-        to = source[n]
-        remote(part.at[to], precv.at[z], p_send.at[n], p_recv.at[z], g, 2 * to + c)
+    def own_side():
+        other_shares()
+        for copy in own_tensor:
+            copy.wait()
+        for q in range(pieces):
+            arrived(tbuf.at[x, q, other], t_side_recv.at[0, q])
+        for j in range(ways):
+            rows_ready(0, j)
+        for j in range(chunks):
+            pending.append((0.5, lambda j=j: window_task(j)))
+        pending.append((0.3, halo_task))
+        pending.append((1.0, lateral_task))
+
+    clock = 3.0
+    agenda.append((clock + 1.0, "own", 0, 0, 0))
+    agenda.sort(key=lambda item: item[0])
+    for when, what, n, s, gap in agenda:
+        while pending and clock + 0.5 * pending[0][0] < when:
+            cost, go = pending.pop(0)
+            go()
+            clock += cost
+        clock = max(clock, when)
+        if what == "rows":
+            rows_event(n, s, gap)
+        elif what == "left":
+            left_event(n)
+        elif what == "side":
+            side_event(n, s)
+            rows_ready(n, s)
+        elif what == "tensor":
+            tensor_event(n)
+        elif what == "tensor_side":
+            tensor_ready(n)
+        elif n:
+            rows_ready(n, 0)
+        else:
+            own_side()
+    for _, go in pending:
+        go()
+
+    arrivals = [(n, kind, j) for n in range(1, line) for kind in range(2) for j in range(ways)]
+    for n, kind, j in arrivals:
+        spot = precv.at[source[n], (x, 1 - x)[kind], share_at(j)]
+        arrived(spot, p_recv.at[source[n], (x, 1 - x)[kind], share_at(j)])
     total = part[z]
     for n in range(1, line):
-        arrived(precv.at[source[n]], p_recv.at[source[n]])
         total = total + precv[source[n]]
     for gx in range(2):
         for yh in range(ways):
@@ -374,9 +442,9 @@
     modes = local_modes * groups
     share = cells // ways
     assert share % PLANE == 0 and width == bricks * depth
-    step = 2 if local_modes % 2 == 0 else 1
+    step = 1
     pieces = local_modes // step
-    subs = share // 64
+    subs = width // PLANE
     chunks = cells // PLANE
     layers = cells // PLANE
     slab = 2 * depth
@@ -385,7 +453,7 @@
     sem = pltpu.SemaphoreType.DMA
     scratch = [
         pltpu.VMEM((2, pieces, 2, step, depth, width), bf16),
-        pltpu.VMEM((line, ways, share, width), bf16),
+        pltpu.VMEM((line, ways, width, share), bf16),
         pltpu.VMEM((line, ways, slab, share), bf16),
         pltpu.VMEM((line, ways, slab, share), bf16),
         pltpu.VMEM((layers + 2, modes, species, PLANE), f32),
@@ -414,8 +482,8 @@
         sem((line, ways)),
         sem((2,)),
         sem((2,)),
-        sem((line,)),
-        sem((line,)),
+        sem((line, 2, ways)),
+        sem((line, 2, ways)),
         sem((3, groups)),
         sem((3, groups)),
     ]
@@ -431,7 +499,7 @@
         ],
         out_specs=pl.BlockSpec(memory_space=pltpu.VMEM),
         scratch_shapes=scratch,
-        compiler_params=pltpu.CompilerParams(has_side_effects=True, vmem_limit_bytes=60 * 2**20),
+        compiler_params=pltpu.CompilerParams(has_side_effects=True, collective_id=0, vmem_limit_bytes=60 * 2**20),
         name="fused",
     )(coeffs, tensor, lateral.reshape(1, cells), pairs, thermal)
 

time: 87.6 us -> 77.7 us (0.89)
  Pallas kernels: 85.3 us -> 75.7 us
    pallas_call x1, Pallas kernels: 85.3 us -> 75.7 us  [local(): pl.pallas_call(lambda *refs: fused_kernel(dims, *refs), out_shape=jax.Sha...]
where the time goes in v1:
time: 77.7 us; the launch traced here: 77.5 us
  Pallas kernels  75.7 us (97%)
  local copies, waits for them, and re-layouts  1.87 us (2%)
    pallas_call x1, Pallas kernels, local(): pl.pallas_call(lambda *refs: fused_kernel(dims, *refs), out_shape=jax.Sha...  75.7 us
    unnamed x1, local copies, waits for them, and re-layouts  1.87 us

profile of v1, /device:TPU:0, one launch (start us, length us, event | category | flops | bytes accessed | tf_op | source)
XLA Modules:
  0.0 77.5 jit_solution(10090003188041657319)
XLA Ops:
  0.0 75.7 %fused.1 = f32[32,8,512]{2,1,0:T(8,128)} custom-call(bf16[8,512,1024]{2,1,0:T(8,128)(2,1)} %refs_0_.1, bf16[8,128,1024]{2,1,0:T(8,128)(2,1)} %refs_1_.1, s32[1,512]{1,0:T(1,128)} %bitcast.1, s32[2,2]{1,0:T(2,128)} %refs_3_.1, f32[8]{0:T(128)} %refs_4_.1), custom_call_target="tpu_custom_call" | custom-call | tf_op jit(solution)/shard_map/fused/pallas_call | solution.py:490
  75.7 1.9 %copy.7 = f32[32,8,512]{2,1,0:T(8,128)} copy(f32[32,8,512]{2,1,0:T(8,128)} %fused.1) | data formatting | bytes 1048576

commit v2 on v1

--- a/solution.py
+++ b/solution.py
@@ -25,8 +25,8 @@
 
 
 def fused_kernel(dims, coeffs_ref, tensor_ref, lateral_ref, pairs_ref, thermal_ref, o_ref, *scratch):
-    (tbuf, rbuf, lbuf, own_left, win, gathered, hot, part, precv, coll) = scratch[:10]
-    views = scratch[10 : 10 + dims["chunks"]]
+    (tbuf, rbuf, lbuf, own_left, win, gathered, hot, part, precv, coll, edge, rim) = scratch[:12]
+    views = scratch[12 : 12 + dims["chunks"]]
     (
         chunk_sem,
         t_local,
@@ -49,7 +49,7 @@
         p_recv,
         c_send,
         c_recv,
-    ) = scratch[10 + dims["chunks"] :]
+    ) = scratch[12 + dims["chunks"] :]
     line, ways, pieces, subs = dims["line"], dims["ways"], dims["pieces"], dims["subs"]
     chunks, bricks = dims["chunks"], 2 * dims["line"]
     local_modes, depth, width = tensor_ref.shape
@@ -59,6 +59,8 @@
     share = cells // ways
     sub = width // subs
     slab = 2 * depth
+    cuts = dims["cuts"]
+    cut = slab // cuts
     layers = cells // PLANE
     per_share = share // PLANE
 
@@ -151,7 +153,16 @@
         for n in range(1, line):
             if slots[n - 1] == s:
                 to = 2 * source[n] + c
-                remote(own_left.at[source[n], y], lbuf.at[z, y], l_send.at[n], l_recv.at[z], g, to)
+                for k in range(cuts):
+                    span = pl.ds(k * cut, cut)
+                    remote(
+                        own_left.at[source[n], y, span],
+                        lbuf.at[z, y, span],
+                        l_send.at[n, k],
+                        l_recv.at[z, k],
+                        g,
+                        to,
+                    )
         piece = rbuf.at[z, y, pl.ds(s * sub, sub)]
         for d, to in enumerate((z - 1, z + 1)):
             remote(
@@ -182,8 +193,10 @@
         gathered[...] = jnp.dot(flat, hot[...], preferred_element_type=jnp.float32).reshape(modes, species, cells)
 
     def halo_task():
-        remote(win.at[1], win.at[layers + 1], h_send.at[0], h_recv.at[0], g, before)
-        remote(win.at[layers], win.at[0], h_send.at[1], h_recv.at[1], g, after)
+        edge[0] = win[1].astype(jnp.bfloat16)
+        edge[1] = win[layers].astype(jnp.bfloat16)
+        remote(edge.at[0], rim.at[1], h_send.at[0], h_recv.at[1], g, before)
+        remote(edge.at[1], rim.at[0], h_send.at[1], h_recv.at[0], g, after)
 
     def contract(gx, q, count, zi, yh):
         halves = []
@@ -225,23 +238,24 @@
     sub_us = piece_us / subs
     agenda = []
     for n in range(1, line):
-        left_at = begin + slots[n - 1] * sub_us + 2 * n * left_us
-        agenda.append((left_at, "left", n, 0, 0))
+        left_at = begin + slots[n - 1] * sub_us + 2 * n * left_us + (2.0 if n > 1 else 0.0)
+        for k in range(cuts):
+            agenda.append((left_at - (cuts - 1 - k) * left_us * 2 / cuts, "left", n, k, 0))
         last = 0.0
         for gap in gaps[n]:
             for s in range(subs):
                 at = begin + (gap - 1) * piece_us + (s + 1) * sub_us
                 if gap == 1:
-                    at += left_us * sum(s >= slot for slot in slots[:2])
+                    at += left_us * sum(s >= slot for slot in slots[:1])
                 elif gap == 2:
                     at += left_us * (2 + (line - 3) * (s + 1) / subs)
                 else:
                     at += left_us * (line - 1)
-                agenda.append((at, "rows", n, s, gap))
-            last = at
+                agenda.append((at + (1.7 if gap > 1 else 0.0), "rows", n, s, gap))
+            last = at + 1.7
         agenda.append((max(last, left_at) + 0.01, "own", n, 0, 0))
         for j in range(1, ways):
-            agenda.append((max(last, left_at) + sub_us + hop + 2.0, "side", n, j, 0))
+            agenda.append((max(last, left_at) + sub_us + hop + 3.0, "side", n, j, 0))
     for q in range(pieces):
         agenda.append((hop + (q + 1) * tensor_us, "tensor", q, 0, 0))
         agenda.append((hop + (q + 1) * tensor_us + side_hop, "tensor_side", q, 0, 0))
@@ -292,17 +306,19 @@
                 piece, piece, r_y_send.at[n, s, j], r_y_recv.at[src, y, s], 2 * share_at(j) + x, b, when=near
             )
 
-    def left_event(n):
+    def left_event(n, k):
         src = source[n]
-        arrived(lbuf.at[src, y], l_recv.at[src])
+        piece = lbuf.at[src, y, pl.ds(k * cut, cut)]
+        arrived(piece, l_recv.at[src, k])
         for j in range(1, ways):
-            remote(lbuf.at[src, y], lbuf.at[src, y], l_y_send.at[n, j], l_y_recv.at[src, y], 2 * share_at(j) + x, b)
+            remote(piece, piece, l_y_send.at[n, j, k], l_y_recv.at[src, y, k], 2 * share_at(j) + x, b)
 
     def side_event(n, j):
         src, yh = source[n], share_at(j)
         for s in range(subs):
             arrived(rbuf.at[src, yh, pl.ds(s * sub, sub)], r_y_recv.at[src, yh, s])
-        arrived(lbuf.at[src, yh], l_y_recv.at[src, yh])
+        for k in range(cuts):
+            arrived(lbuf.at[src, yh, pl.ds(k * cut, cut)], l_y_recv.at[src, yh, k])
 
     def own_side():
         other_shares()
@@ -329,7 +345,7 @@
         if what == "rows":
             rows_event(n, s, gap)
         elif what == "left":
-            left_event(n)
+            left_event(n, s)
         elif what == "side":
             side_event(n, s)
             rows_ready(n, s)
@@ -365,8 +381,9 @@
         remote(coll.at[x, y, 1], coll.at[x, y, layers + 1], c_send.at[1, j], c_recv.at[1, g], to, before)
         remote(coll.at[x, y, layers], coll.at[x, y, 0], c_send.at[2, j], c_recv.at[2, g], to, after)
 
-    arrived(win.at[layers + 1], h_recv.at[0])
-    arrived(win.at[0], h_recv.at[1])
+    for d in range(2):
+        arrived(rim.at[d], h_recv.at[d])
+        win[d * (layers + 1)] = rim[d].astype(jnp.float32)
     for j in range(2 * ways):
         src = lax.rem(g + j, 2 * ways)
         sx, sy = lax.rem(src, 2), lax.div(src, 2)
@@ -448,7 +465,8 @@
     chunks = cells // PLANE
     layers = cells // PLANE
     slab = 2 * depth
-    dims = dict(line=line, ways=ways, pieces=pieces, subs=subs, chunks=chunks)
+    cuts = 4 if slab % 64 == 0 else 1
+    dims = dict(cuts=cuts, line=line, ways=ways, pieces=pieces, subs=subs, chunks=chunks)
     bf16, f32 = jnp.bfloat16, jnp.float32
     sem = pltpu.SemaphoreType.DMA
     scratch = [
@@ -462,6 +480,8 @@
         pltpu.VMEM((line, 2, ways, local_modes, share), f32),
         pltpu.VMEM((line, 2, ways, local_modes, share), f32),
         pltpu.VMEM((2, ways, layers + 2, 2 * local_modes, PLANE), f32),
+        pltpu.VMEM((2, modes, species, PLANE), bf16),
+        pltpu.VMEM((2, modes, species, PLANE), bf16),
     ]
     scratch += [pltpu.VMEM((species, PLANE, width), bf16)] * chunks
     scratch += [
@@ -476,10 +496,10 @@
         sem((line, subs)),
         sem((line, subs, ways)),
         sem((line, ways, subs)),
-        sem((line,)),
-        sem((line,)),
-        sem((line, ways)),
-        sem((line, ways)),
+        sem((line, cuts)),
+        sem((line, cuts)),
+        sem((line, ways, cuts)),
+        sem((line, ways, cuts)),
         sem((2,)),
         sem((2,)),
         sem((line, 2, ways)),

time: 77.7 us -> 76.7 us (0.987)
  Pallas kernels: 75.7 us -> 74.6 us
    pallas_call x1, Pallas kernels: 75.7 us -> 74.6 us  [local(): pl.pallas_call(lambda *refs: fused_kernel(dims, *refs), out_shape=jax.Sha...]
where the time goes in v2:
time: 76.7 us; the launch traced here: 76.5 us
  Pallas kernels  74.6 us (97%)
  local copies, waits for them, and re-layouts  1.87 us (2%)
    pallas_call x1, Pallas kernels, local(): pl.pallas_call(lambda *refs: fused_kernel(dims, *refs), out_shape=jax.Sha...  74.6 us
    unnamed x1, local copies, waits for them, and re-layouts  1.87 us

profile of v2, /device:TPU:0, one launch (start us, length us, event | category | flops | bytes accessed | tf_op | source)
XLA Modules:
  0.0 76.5 jit_solution(6143850392329237922)
XLA Ops:
  0.0 74.6 %fused.1 = f32[32,8,512]{2,1,0:T(8,128)} custom-call(bf16[8,512,1024]{2,1,0:T(8,128)(2,1)} %refs_0_.1, bf16[8,128,1024]{2,1,0:T(8,128)(2,1)} %refs_1_.1, s32[1,512]{1,0:T(1,128)} %bitcast.1, s32[2,2]{1,0:T(2,128)} %refs_3_.1, f32[8]{0:T(128)} %refs_4_.1), custom_call_target="tpu_custom_call" | custom-call | tf_op jit(solution)/shard_map/fused/pallas_call | solution.py:510
  74.6 1.9 %copy.7 = f32[32,8,512]{2,1,0:T(8,128)} copy(f32[32,8,512]{2,1,0:T(8,128)} %fused.1) | data formatting | bytes 1048576
